TPU v7x, 256 devices: a whole 4x4x8 slice. The times are simulated.
256 devices in a mesh: ep: 64 (over z, x, core), tp: 4 (over y).
Axes of the slice: x: 4, y: 4, z: 8, core: 2. Of those that a mesh axis runs over, the one named last changes fastest.
Arguments:
- tokens: bfloat16 [16384, 2048], P('ep', 'tp'), may hold values from -180 to 180
- norm_gain: float32 [2048], replicated, may hold values from 0.1 to 1.9
- router_weight: bfloat16 [2048, 60], P('tp'), may hold values from -2 to 2
- shared_gate_w: bfloat16 [2048], replicated, may hold values from -0.125 to 0.125
- expert_ids: int32 [16384, 4], P('ep'), may hold values from 0 to 59, all different within a row; in each aligned block of 256 rows (0 to 255, 256 to 511, ...) at most 32 rows name the same one
- w_gate: bfloat16 [64, 2048, 1408], P('ep', None, 'tp'), may hold values from -0.125 to 0.125
- w_up: bfloat16 [64, 2048, 1408], P('ep', None, 'tp'), may hold values from -0.125 to 0.125
- w_down: bfloat16 [64, 1408, 2048], P('ep', 'tp'), may hold values from -1.5 to 1.5
- shared_w_gate: bfloat16 [2048, 2816], P(None, 'tp'), may hold values from -0.125 to 0.125
- shared_w_up: bfloat16 [2048, 2816], P(None, 'tp'), may hold values from -0.125 to 0.125
- shared_w_down: bfloat16 [2816, 2048], P('tp'), may hold values from -0.109375 to 0.109375
Outputs:
- moe_out: bfloat16 [16384, 2048], P('ep', 'tp')
Inputs may be any that keep to these rules, and one draw needn't show every extreme that they name: `expert_ids`: each row names 4 different experts below 60. Within the 256 rows of one index of ep no expert is named by more than 32 rows, and in some of these blocks one expert is named by exactly 32 rows.
All inputs are finite; a program needn't handle non-finite values.
Results may differ from a plain program's by a relative error of at most 0.0069.
Values may be sent and summed in bfloat16 or wider, within the bound.
No kernel may reach another device: no remote copies, remote signals or barrier semaphores. Data moves between devices by JAX's collectives and lax.ppermute only.
A program may use at most 128 MiB of HBM per device.

v0:
```python
import jax
import jax.numpy as jnp
from jax import lax
from jax.sharding import PartitionSpec as P


def laid_out(parts, dim):
    lengths = list(parts.shape[1:])
    lengths[dim] *= parts.shape[0]
    return jnp.moveaxis(parts, 0, dim).reshape(lengths)


def copy_for_each(value, axis):
    peers = lax.axis_size(axis)
    return lax.all_to_all(
        jnp.broadcast_to(value[None], (peers, *value.shape)), axis, 0, 0, tiled=True
    )


def collect(value, axis, dim):
    return laid_out(copy_for_each(value, axis), dim)


def taken_together(value, axis):
    return copy_for_each(value, axis).sum(axis=0)


def turned_gather(arrays, axis, dims):
    turned = [jnp.moveaxis(a, dim, 0) for a, dim in zip(arrays, dims)]
    both = jnp.concatenate([t.reshape(len(t), -1) for t in turned], axis=1)
    out, at, done = (lax.all_gather(both, axis, axis=0, tiled=True), 0, [])
    for t, dim in zip(turned, dims):
        piece = out[:, at : at + t[0].size].reshape(-1, *t.shape[1:])
        done.append(jnp.moveaxis(piece, 0, dim))
        at += t[0].size
    return tuple(done)


def cut_along(value, dim, peers):
    before, after = (value.shape[:dim], value.shape[dim + 1 :])
    return jnp.moveaxis(value.reshape(*before, peers, -1, *after), dim, 0)


def sent_and_summed(value, axis, dim):
    peers = lax.axis_size(axis)
    parts = lax.all_to_all(cut_along(value, dim, peers), axis, 0, 0, tiled=True)
    return jnp.sum(parts.astype(jnp.float32), axis=0)


def send_back(summed):
    return lax.all_to_all(summed, "ep", split_axis=0, concat_axis=0, tiled=True)


def expert_rows(arrived, w_gate, w_up, w_down):
    share = arrived.shape[0] // lax.axis_size("tp")
    mine = lax.dynamic_slice_in_dim(arrived, lax.axis_index("tp") * share, share, 0)
    gate_act = jnp.einsum("sekd,edf->sekf", mine, w_gate, preferred_element_type=jnp.float32)
    up_act = jnp.einsum("sekd,edf->sekf", mine, w_up, preferred_element_type=jnp.float32)
    hidden = (jax.nn.silu(gate_act) * up_act).astype(jnp.bfloat16)
    full_out = jnp.einsum(
        "sekf,efd->sekd", hidden, w_down, preferred_element_type=jnp.float32
    ).astype(jnp.bfloat16)
    summed = lax.all_to_all(full_out, "tp", split_axis=3, concat_axis=0, tiled=True)
    return send_back(summed)


def per_device(
    tokens,
    norm_gain,
    router_weight,
    shared_gate_w,
    expert_ids,
    w_gate,
    w_up,
    w_down,
    shared_w_gate,
    shared_w_up,
    shared_w_down,
):
    width = tokens.shape[1]
    tok_rows = tokens.shape[0]
    column_start = lax.axis_index("tp") * width
    whole = collect(tokens, "tp", 1)
    values = whole.astype(jnp.float32)
    inv_rms = lax.rsqrt(jnp.mean(values * values, axis=-1, keepdims=True) + 1e-06)
    normed = (values * inv_rms * norm_gain[None, :]).astype(jnp.bfloat16)
    own_part = lax.dynamic_slice_in_dim(normed, column_start, width, 1)
    partial_logits = jnp.dot(own_part, router_weight, preferred_element_type=jnp.float32)
    logits = taken_together(partial_logits, "tp")
    probs = jax.nn.softmax(logits, axis=-1)
    expert_count = logits.shape[1]
    matches = expert_ids[:, :, None] == jnp.arange(expert_count, dtype=jnp.int32)[None, None, :]
    route_weight = jnp.sum(jnp.where(matches, probs[:, None, :], 0.0), axis=-1)
    gate_whole, up_whole = turned_gather((w_gate, w_up), "tp", (2, 2))
    down_whole = lax.all_gather(w_down, "tp", axis=1, tiled=True)
    experts_here = w_gate.shape[0]
    slot_count = lax.axis_size("ep") * experts_here
    capacity = tok_rows // 8
    flat_ids = expert_ids.reshape(-1)
    one_hot = (flat_ids[:, None] == jnp.arange(slot_count, dtype=jnp.int32)[None, :]).astype(
        jnp.int32
    )
    before = jnp.cumsum(one_hot, axis=0) - one_hot
    order_rank = jnp.sum(before * one_hot, axis=1)
    slot_ids = (flat_ids * capacity + order_rank).reshape(expert_ids.shape)
    targets = jnp.arange(slot_count * capacity, dtype=jnp.int32)
    dispatch_map = jnp.sum(
        (slot_ids[None, :, :] == targets[:, None, None]).astype(jnp.bfloat16), axis=2
    )
    outgoing = jnp.dot(dispatch_map, normed, preferred_element_type=jnp.float32).astype(
        jnp.bfloat16
    )
    outgoing = outgoing.reshape(lax.axis_size("ep"), experts_here, capacity, normed.shape[1])
    returned = expert_rows(
        lax.all_to_all(outgoing, "ep", split_axis=0, concat_axis=0, tiled=True),
        w_gate=gate_whole,
        w_up=up_whole,
        w_down=down_whole,
    )
    picked = returned.reshape(slot_count * capacity, width)[slot_ids]
    routed = jnp.sum(route_weight[:, :, None] * picked.astype(jnp.float32), axis=1)
    shared_gate_act = jnp.dot(normed, shared_w_gate, preferred_element_type=jnp.float32)
    shared_up_act = jnp.dot(normed, shared_w_up, preferred_element_type=jnp.float32)
    shared_hidden = (jax.nn.silu(shared_gate_act) * shared_up_act).astype(jnp.bfloat16)
    shared_part = jnp.dot(shared_hidden, shared_w_down, preferred_element_type=jnp.float32)
    shared_own = sent_and_summed(shared_part.astype(jnp.bfloat16), "tp", 1)
    share_gate = jax.nn.sigmoid(jnp.dot(normed, shared_gate_w, preferred_element_type=jnp.float32))
    return (share_gate[:, None] * shared_own + routed).astype(jnp.bfloat16)


def solution(mesh):
    return jax.shard_map(
        per_device,
        mesh=mesh,
        in_specs=(
            P("ep", "tp"),
            P(),
            P("tp", None),
            P(),
            P("ep", None),
            P("ep", None, "tp"),
            P("ep", None, "tp"),
            P("ep", "tp", None),
            P(None, "tp"),
            P(None, "tp"),
            P("tp", None),
        ),
        out_specs=P("ep", "tp"),
        check_vma=False,
    )
```

profile of v0, /device:TPU:8, one launch (start us, length us, event | category | flops | bytes accessed | tf_op | source)
XLA Modules:
  0.0 429.5 jit_solution(3899483268526843282)
XLA Ops:
  12.5 6.4 %all-to-all-start = ((bf16[4,256,512]{1,2,0:T(8,128)(2,1)}), bf16[4,256,512]{1,2,0:T(8,128)(2,1)}, u32[]{:S(2)}, u32[]{:S(2)}) async-start(bf16[4,256,512]{1,2,0:T(8,128)(2,1)} %broadcast_in_dim.14), calls=%async_computation | async-start | bytes 2097152 | tf_op jit(solution)/shard_map/all_to_all | solution.py:15
  19.2 18.0 %reduce-window.6 = s32[64,8,128]{2,1,0:T(8,128)S(1)} reduce-window(s32[64,8,128]{2,1,0:T(8,128)S(1)} %fusion.47, s32[]{:T(128)} %constant.8.clone.1), window={size=1x1x128 pad=0_0x0_0x127_0}, to_apply=%region_6.7 | reduce-window | flops 8323072 | bytes 524292 | tf_op jit(solution)/shard_map/reduce-window
  43.9 5.8 %convolution_convert_fusion = bf16[2048,2048]{1,0:T(8,128)(2,1)} fusion(bf16[2048,256]{1,0:T(8,128)(2,1)S(1)} %copy-done.2, bf16[256,2048]{0,1:T(8,128)(2,1)S(1)} %fusion.32), kind=kOutput, calls=%fused_computation.3 | convolution fusion | flops 2151677952 | bytes 10485760 | tf_op jit(solution)/shard_map/dot_general | solution.py:110
  49.7 10.9 %all-to-all-start.3 = ((bf16[64,1,32,2048]{3,2,1,0:T(8,128)(2,1)}), bf16[64,1,32,2048]{3,2,1,0:T(8,128)(2,1)}, u32[]{:S(2)}, u32[]{:S(2)}) async-start(bf16[64,1,32,2048]{3,2,1,0:T(8,128)(2,1)} %bitcast.131), calls=%async_computation.3 | async-start | bytes 16777216 | tf_op jit(solution)/shard_map/all_to_all | solution.py:115
  62.5 63.2 %all-gather.3.cloned.1.call-done = bf16[1408,4096]{1,0:T(8,128)(2,1)} async-done(((bf16[352,4096]{1,0:T(8,128)(2,1)}), bf16[1408,4096]{1,0:T(8,128)(2,1)}) %all-gather.3.cloned.1.call-update) | async-done | bytes 11534352 | tf_op jit(solution)/shard_map/all_gather | solution.py:31
  125.7 11.0 %fusion.56 = (bf16[1408,2048]{1,0:T(8,128)(2,1)}, bf16[1408,2048]{1,0:T(8,128)(2,1)}) fusion(bf16[1408,4096]{1,0:T(8,128)(2,1)} %all-gather.3.cloned.1.call-done), kind=kLoop, calls=%fused_computation.61 | loop fusion | bytes 23068672 | tf_op jit(solution)/shard_map/slice | solution.py:33
  136.6 8.5 %copy.110 = bf16[1408,2048]{0,1:T(8,128)(2,1)} copy(bf16[1408,2048]{1,0:T(8,128)(2,1)} %get-tuple-element.7) | data formatting | bytes 11534336
  145.2 8.4 %copy.111 = bf16[1408,2048]{0,1:T(8,128)(2,1)} copy(bf16[1408,2048]{1,0:T(8,128)(2,1)} %get-tuple-element.8) | data formatting | bytes 11534336
  153.5 93.2 %all-to-all-done.3 = bf16[64,1,32,2048]{3,2,1,0:T(8,128)(2,1)} async-done(((bf16[64,1,32,2048]{3,2,1,0:T(8,128)(2,1)}), bf16[64,1,32,2048]{3,2,1,0:T(8,128)(2,1)}, u32[]{:S(2)}, u32[]{:S(2)}) %all-to-all-start.3) | async-done | bytes 8388640 | tf_op jit(solution)/shard_map/all_to_all | solution.py:115
  247.5 4.8 %all-to-all-start.2 = ((f32[4,256,60]{1,2,0:T(8,128)}), f32[4,256,60]{1,2,0:T(8,128)S(1)}, u32[]{:S(2)}, u32[]{:S(2)}) async-start(f32[4,256,60]{1,2,0:T(8,128)} %broadcast_in_dim.15), calls=%async_computation.2 | async-start | bytes 524288 | tf_op jit(solution)/shard_map/all_to_all | solution.py:15
  252.3 8.3 %fusion.8 = f32[16,1,32,1408]{3,2,0,1:T(8,128)} fusion(bf16[1408,2048]{0,1:T(8,128)(2,1)} %copy.110, bf16[64,1,32,2048]{3,2,1,0:T(8,128)(2,1)} %all-to-all-done.3, s32[]{:T(128)S(6)} %select_n.15), kind=kOutput, calls=%fused_computation.11 | convolution fusion | flops 2952790016 | bytes 10747908 | tf_op jit(solution)/shard_map/sekd,edf->sekf/dot_general | solution.py:57
  260.6 14.2 %fusion.23 = bf16[16,1,32,2048]{3,2,0,1:T(8,128)(2,1)} fusion(bf16[1,1408,2048]{2,1,0:T(8,128)(2,1)} %all-gather.5.cloned.1.call-done, bf16[1408,2048]{0,1:T(8,128)(2,1)} %copy.111, f32[16,1,32,1408]{3,2,0,1:T(8,128)} %fusion.8, bf16[64,1,32,2048]{3,2,1,0:T(8,128)(2,1)} %all-to-all-done.3, s32[]{:T(128)S(6)} %select_n.15), kind=kOutput, calls=%fused_computation.17 | convolution fusion | flops 5910953984 | bytes 18612228 | tf_op jit(solution)/shard_map/sekf,efd->sekd/dot_general | solution.py:60
  274.8 9.9 %copy.104 = bf16[16,1,32,2048]{2,0,1,3:T(8,128)(2,1)} copy(bf16[16,1,32,2048]{3,2,0,1:T(8,128)(2,1)} %fusion.23) | data formatting | bytes 4194304 | tf_op jit(solution)/shard_map/convert_element_type | solution.py:62
  284.7 10.6 %reshape.141 = bf16[4,2,131072]{2,1,0:T(2,128)(2,1)} reshape(bf16[2048,1,16,32]{3,2,1,0:T(8,128)(2,1)} %bitcast.132) | data formatting | bytes 4194304
  295.3 4.8 %all-to-all-start.4 = ((bf16[4,2,131072]{2,1,0:T(2,128)(2,1)}), bf16[4,2,131072]{2,1,0:T(2,128)(2,1)}, u32[]{:S(2)}, u32[]{:S(2)}) async-start(bf16[4,2,131072]{2,1,0:T(2,128)(2,1)} %reshape.141), calls=%async_computation.4 | async-start | bytes 4194304 | tf_op jit(solution)/shard_map/all_to_all | solution.py:63
  300.1 3.9 fusion.58
  304.0 6.5 %convolution_convert_fusion.1 = bf16[256,2048]{1,0:T(8,128)(2,1)} fusion(bf16[704,2048]{1,0:T(8,128)(2,1)S(1)} %copy-done, bf16[2048,704]{0,1:T(8,128)(2,1)} %param.20, bf16[256,2048]{0,1:T(8,128)(2,1)} %copy-done.1, f32[256,704]{0,1:T(8,128)} %fusion.58), kind=kOutput, calls=%fused_computation.19 | convolution fusion | flops 1478000640 | bytes 8585216 | tf_op jit(solution)/shard_map/dot_general | solution.py:125
  312.9 8.3 %all-to-all-done.4 = bf16[4,2,131072]{2,1,0:T(2,128)(2,1)} async-done(((bf16[4,2,131072]{2,1,0:T(2,128)(2,1)}), bf16[4,2,131072]{2,1,0:T(2,128)(2,1)}, u32[]{:S(2)}, u32[]{:S(2)}) %all-to-all-start.4) | async-done | bytes 2097184 | tf_op jit(solution)/shard_map/all_to_all | solution.py:63
  321.1 5.7 %all-to-all-start.1 = ((bf16[4,256,512]{2,1,0:T(8,128)(2,1)}), bf16[4,256,512]{2,1,0:T(8,128)(2,1)}, u32[]{:S(2)}, u32[]{:S(2)}) async-start(bf16[4,256,512]{2,1,0:T(8,128)(2,1)} %bitcast.136), calls=%async_computation.1 | async-start | bytes 2097152 | tf_op jit(solution)/shard_map/all_to_all | solution.py:46
  326.8 7.4 %reshape.142 = bf16[2048,1,16,32]{3,2,1,0:T(8,128)(2,1)} reshape(bf16[4,2,131072]{2,1,0:T(2,128)(2,1)} %all-to-all-done.4) | data formatting | bytes 4194304
  334.2 9.9 %copy.109 = bf16[16,1,32,4,512]{4,3,2,0,1:T(4,128)(2,1)} copy(bf16[16,1,32,4,512]{2,0,4,3,1:T(8,128)(2,1)} %bitcast.133) | data formatting | bytes 4194304 | tf_op jit(solution)/shard_map/all_to_all | solution.py:63
  347.6 10.4 %all-to-all-start.5 = ((bf16[64,1,32,512]{3,2,1,0:T(8,128)(2,1)}), bf16[64,1,32,512]{3,2,1,0:T(8,128)(2,1)}, u32[]{:S(2)}, u32[]{:S(2)}) async-start(bf16[64,1,32,512]{3,2,1,0:T(8,128)(2,1)} %bitcast.135), calls=%async_computation.5 | async-start | bytes 4194304 | tf_op jit(solution)/shard_map/all_to_all | solution.py:51
  361.6 47.6 %all-to-all-done.5 = bf16[64,1,32,512]{3,2,1,0:T(8,128)(2,1)} async-done(((bf16[64,1,32,512]{3,2,1,0:T(8,128)(2,1)}), bf16[64,1,32,512]{3,2,1,0:T(8,128)(2,1)}, u32[]{:S(2)}, u32[]{:S(2)}) %all-to-all-start.5) | async-done | bytes 2097184 | tf_op jit(solution)/shard_map/all_to_all | solution.py:51
  409.1 7.0 %gather_fusion = bf16[1024,512]{1,0:T(8,128)(2,1)} fusion(bf16[2048,512]{1,0:T(8,128)(2,1)} %bitcast.36, s32[1024]{0:T(1024)S(1)} %broadcast_clamp_fusion), kind=kCustom, calls=%fused_computation | custom fusion | bytes 2101248 | tf_op jit(solution)/shard_map/gather | solution.py:120
  (65 shorter events, 31.4 us)
Async XLA Ops:
  6.5 297.4 %copy-start = (bf16[704,2048]{1,0:T(8,128)(2,1)S(1)}, bf16[704,2048]{1,0:T(8,128)(2,1)}, u32[]{:S(2)}) copy-start(bf16[704,2048]{1,0:T(8,128)(2,1)} %param.21) | copy-start | bytes 8650756
  6.5 119.1 %all-gather.3.cloned.1.call-start = ((), (), s32[]{:S(2)}) async-start(), calls=%async_computation.6 | async-start | bytes 14417920 | tf_op jit(solution)/shard_map/all_gather | solution.py:31
  10.3 0.9 copy-start.3
  10.4 8.5 %copy-start.5 = (s32[256,4]{0,1:T(4,128)S(1)}, s32[256,4]{0,1:T(4,128)}, u32[]{:S(2)}) copy-start(s32[256,4]{0,1:T(4,128)} %param.15) | copy-start | bytes 12292
  12.5 28.2 %all-to-all-start = ((bf16[4,256,512]{1,2,0:T(8,128)(2,1)}), bf16[4,256,512]{1,2,0:T(8,128)(2,1)}, u32[]{:S(2)}, u32[]{:S(2)}) async-start(bf16[4,256,512]{1,2,0:T(8,128)(2,1)} %broadcast_in_dim.14), calls=%async_computation | async-start | bytes 2097152 | tf_op jit(solution)/shard_map/all_to_all | solution.py:15
  18.8 23.5 %copy-start.6 = (f32[2048]{0:T(1024)S(1)}, f32[2048]{0:T(1024)}, u32[]{:S(2)}) copy-start(f32[2048]{0:T(1024)} %param.12) | copy-start | bytes 24580
  40.7 3.2 copy-start.2
  43.9 5.8 %copy-start.1 = (bf16[256,2048]{0,1:T(8,128)(2,1)}, bf16[256,2048]{0,1:T(8,128)(2,1)S(1)}, u32[]{:S(2)}) copy-start(bf16[256,2048]{0,1:T(8,128)(2,1)S(1)} %fusion.32) | copy-start | bytes 3145732
  49.7 11.7 %copy-start.4 = (bf16[512,60]{0,1:T(8,128)(2,1)S(1)}, bf16[512,60]{0,1:T(8,128)(2,1)}, u32[]{:S(2)}) copy-start(bf16[512,60]{0,1:T(8,128)(2,1)} %param.13) | copy-start | bytes 184324
  49.7 197.1 %all-to-all-start.3 = ((bf16[64,1,32,2048]{3,2,1,0:T(8,128)(2,1)}), bf16[64,1,32,2048]{3,2,1,0:T(8,128)(2,1)}, u32[]{:S(2)}, u32[]{:S(2)}) async-start(bf16[64,1,32,2048]{3,2,1,0:T(8,128)(2,1)} %bitcast.131), calls=%async_computation.3 | async-start | bytes 16777216 | tf_op jit(solution)/shard_map/all_to_all | solution.py:115
  60.6 200.0 %all-gather.5.cloned.1.call-start = ((), (), s32[]{:S(2)}) async-start(), calls=%async_computation.7 | async-start | bytes 7208960 | tf_op jit(solution)/shard_map/all_gather | solution.py:95
  247.5 47.8 %all-to-all-start.2 = ((f32[4,256,60]{1,2,0:T(8,128)}), f32[4,256,60]{1,2,0:T(8,128)S(1)}, u32[]{:S(2)}, u32[]{:S(2)}) async-start(f32[4,256,60]{1,2,0:T(8,128)} %broadcast_in_dim.15), calls=%async_computation.2 | async-start | bytes 524288 | tf_op jit(solution)/shard_map/all_to_all | solution.py:15
  295.3 25.9 %all-to-all-start.4 = ((bf16[4,2,131072]{2,1,0:T(2,128)(2,1)}), bf16[4,2,131072]{2,1,0:T(2,128)(2,1)}, u32[]{:S(2)}, u32[]{:S(2)}) async-start(bf16[4,2,131072]{2,1,0:T(2,128)(2,1)} %reshape.141), calls=%async_computation.4 | async-start | bytes 4194304 | tf_op jit(solution)/shard_map/all_to_all | solution.py:63
  321.1 26.4 %all-to-all-start.1 = ((bf16[4,256,512]{2,1,0:T(8,128)(2,1)}), bf16[4,256,512]{2,1,0:T(8,128)(2,1)}, u32[]{:S(2)}, u32[]{:S(2)}) async-start(bf16[4,256,512]{2,1,0:T(8,128)(2,1)} %bitcast.136), calls=%async_computation.1 | async-start | bytes 2097152 | tf_op jit(solution)/shard_map/all_to_all | solution.py:46
  347.6 10.6 %copy-start.7 = (bf16[2048]{0:T(1024)(128)(2,1)S(1)}, bf16[2048]{0:T(1024)(128)(2,1)}, u32[]{:S(2)}) copy-start(bf16[2048]{0:T(1024)(128)(2,1)} %param.14) | copy-start | bytes 12292
  347.6 61.6 %all-to-all-start.5 = ((bf16[64,1,32,512]{3,2,1,0:T(8,128)(2,1)}), bf16[64,1,32,512]{3,2,1,0:T(8,128)(2,1)}, u32[]{:S(2)}, u32[]{:S(2)}) async-start(bf16[64,1,32,512]{3,2,1,0:T(8,128)(2,1)} %bitcast.135), calls=%async_computation.5 | async-start | bytes 4194304 | tf_op jit(solution)/shard_map/all_to_all | solution.py:51
Sparse Core Ops, SparseCore 0:
  10.5 115.1 all-gather.2
  127.5 64.4 all-gather.4
where the time goes:
time: 431 us; the launch traced here: 429 us
  waiting for transfers between devices  213 us (49%)
  local copies, waits for them, and re-layouts  85.4 us (20%)
  starting transfers between devices  42.9 us (10%)
  matrix products  41.3 us (10%)
  other arithmetic  33.3 us (8%)
  between operations  13.6 us (3%)
    all_to_all x1, waiting for transfers between devices, per_device(): lax.all_to_all(outgoing, 'ep', split_axis=0, concat_axis=0, tiled=True)  93.2 us
    all_gather x1, waiting for transfers between devices, turned_gather(): out, at, done = (lax.all_gather(both, axis, axis=0, tiled=True), 0, [])  63.2 us
    all_to_all x1, waiting for transfers between devices, send_back(): return lax.all_to_all(summed, 'ep', split_axis=0, concat_axis=0, tiled=True)  47.6 us
    unnamed x23, local copies, waits for them, and re-layouts  36.1 us
    another operation x3, other arithmetic  18.2 us
    dot_general x1, matrix products, expert_rows(): jnp.einsum('sekf,efd->sekd', hidden, w_down, preferred_element_type=jnp.f...  14.2 us
    all_to_all x2, local copies, waits for them, and re-layouts, expert_rows(): lax.all_to_all(full_out, 'tp', split_axis=3, concat_axis=0, tiled=True)  13.4 us
    all_to_all x2, starting transfers between devices, copy_for_each(): lax.all_to_all(jnp.broadcast_to(value[None], (peers, *value.shape)), axis...  11.2 us
  transfers between devices with their start and end apart: 8, of which 4 were waited for; matrix products, arithmetic and copies ran while one was open for 33% of the time, Pallas kernels for 0%

commit v1 on v0

--- a/solution.py
+++ b/solution.py
@@ -2,6 +2,22 @@
 import jax.numpy as jnp
 from jax import lax
 from jax.sharding import PartitionSpec as P
+
+
+def swapped_with_each(x, axis, split, join):
+    ways, here = (lax.axis_size(axis), lax.axis_index(axis))
+    width = x.shape[split] // ways
+    shape = list(x.shape)
+    shape[split] = width
+    height = shape[join]
+    shape[join] = height * ways
+    full = jnp.zeros(shape, x.dtype)
+    for mask in range(ways):
+        part = lax.dynamic_slice_in_dim(x, (here ^ mask) * width, width, axis=split)
+        if mask:
+            part = lax.ppermute(part, axis, [(d, d ^ mask) for d in range(ways)])
+        full = lax.dynamic_update_slice_in_dim(full, part, (here ^ mask) * height, axis=join)
+    return full
 
 
 def laid_out(parts, dim):
@@ -60,7 +76,7 @@
     full_out = jnp.einsum(
         "sekf,efd->sekd", hidden, w_down, preferred_element_type=jnp.float32
     ).astype(jnp.bfloat16)
-    summed = lax.all_to_all(full_out, "tp", split_axis=3, concat_axis=0, tiled=True)
+    summed = swapped_with_each(full_out, "tp", 3, 0)
     return send_back(summed)
 
 

time: 431 us -> 406 us (0.942)
  local copies, waits for them, and re-layouts: 85.4 us -> 55.8 us
    unnamed x23 -> x21, local copies, waits for them, and re-layouts: 36.1 us -> 18.1 us
    all_to_all x2 -> x0, local copies, waits for them, and re-layouts: 13.4 us -> none  [expert_rows(): lax.all_to_all(full_out, 'tp', split_axis=3, concat_axis=0, tiled=True)]
    ppermute x0 -> x3, waiting for transfers between devices: none -> 13 us  [swapped_with_each(): part = lax.ppermute(part, axis, [(d, d ^ mask) for d in range(ways)])]
    convert_element_type x1 -> x0, local copies, waits for them, and re-layouts: 9.95 us -> none  [expert_rows(): full_out = jnp.einsum('sekf,efd->sekd', hidden, w_down, preferred_element...]
    all_to_all x1 -> x0, waiting for transfers between devices: 8.27 us -> none  [expert_rows(): lax.all_to_all(full_out, 'tp', split_axis=3, concat_axis=0, tiled=True)]
    dynamic_update_slice x0 -> x4, local copies, waits for them, and re-layouts: none -> 7.56 us  [swapped_with_each(): lax.dynamic_update_slice_in_dim(full, part, (here ^ mask) * height, axis=...]
    all_to_all x1 -> x0, starting transfers between devices: 4.8 us -> none  [expert_rows(): lax.all_to_all(full_out, 'tp', split_axis=3, concat_axis=0, tiled=True)]
  transfers between devices with their start and end apart: 8 -> 10, of which waited for: 4 -> 6; matrix products, arithmetic and copies ran while one was open for 33% -> 28% of each run, Pallas kernels for 0% -> 0%
where the time goes in v1:
time: 406 us; the launch traced here: 402 us
  waiting for transfers between devices  215 us (53%)
  local copies, waits for them, and re-layouts  55.8 us (14%)
  starting transfers between devices  43.7 us (11%)
  matrix products  41.3 us (10%)
  other arithmetic  33.3 us (8%)
  between operations  13.7 us (3%)
    all_to_all x1, waiting for transfers between devices, per_device(): lax.all_to_all(outgoing, 'ep', split_axis=0, concat_axis=0, tiled=True)  93.2 us
    all_gather x1, waiting for transfers between devices, turned_gather(): out, at, done = (lax.all_gather(both, axis, axis=0, tiled=True), 0, [])  59.2 us
    all_to_all x1, waiting for transfers between devices, send_back(): return lax.all_to_all(summed, 'ep', split_axis=0, concat_axis=0, tiled=True)  47.6 us
    another operation x3, other arithmetic  18.2 us
    unnamed x21, local copies, waits for them, and re-layouts  18.1 us
    dot_general x1, matrix products, expert_rows(): jnp.einsum('sekf,efd->sekd', hidden, w_down, preferred_element_type=jnp.f...  14.1 us
    ppermute x3, waiting for transfers between devices, swapped_with_each(): part = lax.ppermute(part, axis, [(d, d ^ mask) for d in range(ways)])  13 us
    all_to_all x1, starting transfers between devices, send_back(): return lax.all_to_all(summed, 'ep', split_axis=0, concat_axis=0, tiled=True)  12.4 us
  transfers between devices with their start and end apart: 10, of which 6 were waited for; matrix products, arithmetic and copies ran while one was open for 28% of the time, Pallas kernels for 0%

profile of v1, /device:TPU:8, one launch (start us, length us, event | category | flops | bytes accessed | tf_op | source)
XLA Modules:
  0.0 402.4 jit_solution(17261211205655108749)
XLA Ops:
  6.5 3.8 pad_maximum_fusion
  12.5 6.4 %all-to-all-start = ((bf16[4,256,512]{1,2,0:T(8,128)(2,1)}), bf16[4,256,512]{1,2,0:T(8,128)(2,1)}, u32[]{:S(2)}, u32[]{:S(2)}) async-start(bf16[4,256,512]{1,2,0:T(8,128)(2,1)} %broadcast_in_dim.16), calls=%async_computation | async-start | bytes 2097152 | tf_op jit(solution)/shard_map/all_to_all | solution.py:31
  19.2 18.0 %reduce-window.6 = s32[64,8,128]{2,1,0:T(8,128)S(1)} reduce-window(s32[64,8,128]{2,1,0:T(8,128)S(1)} %fusion.44, s32[]{:T(128)} %constant.20.clone.1), window={size=1x1x128 pad=0_0x0_0x127_0}, to_apply=%region_6.7 | reduce-window | flops 8323072 | bytes 524292 | tf_op jit(solution)/shard_map/reduce-window
  43.9 5.8 %convolution_convert_fusion = bf16[2048,2048]{1,0:T(8,128)(2,1)} fusion(bf16[2048,256]{1,0:T(8,128)(2,1)S(1)} %copy-done.2, bf16[256,2048]{0,1:T(8,128)(2,1)S(1)} %fusion.29), kind=kOutput, calls=%fused_computation.3 | convolution fusion | flops 2151677952 | bytes 10485760 | tf_op jit(solution)/shard_map/dot_general | solution.py:126
  49.7 10.9 %all-to-all-start.3 = ((bf16[64,1,32,2048]{3,2,1,0:T(8,128)(2,1)}), bf16[64,1,32,2048]{3,2,1,0:T(8,128)(2,1)}, u32[]{:S(2)}, u32[]{:S(2)}) async-start(bf16[64,1,32,2048]{3,2,1,0:T(8,128)(2,1)} %bitcast.148), calls=%async_computation.3 | async-start | bytes 16777216 | tf_op jit(solution)/shard_map/all_to_all | solution.py:131
  62.5 3.9 fusion.55
  66.4 59.2 %all-gather.3.cloned.1.call-done = bf16[1408,4096]{1,0:T(8,128)(2,1)} async-done(((bf16[352,4096]{1,0:T(8,128)(2,1)}), bf16[1408,4096]{1,0:T(8,128)(2,1)}) %all-gather.3.cloned.1.call-update) | async-done | bytes 11534352 | tf_op jit(solution)/shard_map/all_gather | solution.py:47
  125.7 11.0 %fusion.53 = (bf16[1408,2048]{1,0:T(8,128)(2,1)}, bf16[1408,2048]{1,0:T(8,128)(2,1)}) fusion(bf16[1408,4096]{1,0:T(8,128)(2,1)} %all-gather.3.cloned.1.call-done), kind=kLoop, calls=%fused_computation.67 | loop fusion | bytes 23068672 | tf_op jit(solution)/shard_map/slice | solution.py:49
  136.6 8.5 %copy.94 = bf16[1408,2048]{0,1:T(8,128)(2,1)} copy(bf16[1408,2048]{1,0:T(8,128)(2,1)} %get-tuple-element.7) | data formatting | bytes 11534336
  145.2 8.4 %copy.95 = bf16[1408,2048]{0,1:T(8,128)(2,1)} copy(bf16[1408,2048]{1,0:T(8,128)(2,1)} %get-tuple-element.8) | data formatting | bytes 11534336
  153.5 93.2 %all-to-all-done.3 = bf16[64,1,32,2048]{3,2,1,0:T(8,128)(2,1)} async-done(((bf16[64,1,32,2048]{3,2,1,0:T(8,128)(2,1)}), bf16[64,1,32,2048]{3,2,1,0:T(8,128)(2,1)}, u32[]{:S(2)}, u32[]{:S(2)}) %all-to-all-start.3) | async-done | bytes 8388640 | tf_op jit(solution)/shard_map/all_to_all | solution.py:131
  247.5 4.8 %all-to-all-start.2 = ((f32[4,256,60]{1,2,0:T(8,128)}), f32[4,256,60]{1,2,0:T(8,128)S(1)}, u32[]{:S(2)}, u32[]{:S(2)}) async-start(f32[4,256,60]{1,2,0:T(8,128)} %broadcast_in_dim.17), calls=%async_computation.2 | async-start | bytes 524288 | tf_op jit(solution)/shard_map/all_to_all | solution.py:31
  252.3 8.3 %fusion.8 = f32[16,1,32,1408]{3,2,0,1:T(8,128)} fusion(bf16[1408,2048]{0,1:T(8,128)(2,1)} %copy.94, bf16[64,1,32,2048]{3,2,1,0:T(8,128)(2,1)} %all-to-all-done.3, s32[]{:T(128)S(6)} %select_n.35), kind=kOutput, calls=%fused_computation.11 | convolution fusion | flops 2952790016 | bytes 10747908 | tf_op jit(solution)/shard_map/sekd,edf->sekf/dot_general | solution.py:73
  260.6 14.1 %fusion.17 = bf16[16,32,2048]{2,1,0:T(8,128)(2,1)} fusion(bf16[1,1408,2048]{2,1,0:T(8,128)(2,1)} %all-gather.5.cloned.1.call-done, bf16[1408,2048]{0,1:T(8,128)(2,1)} %copy.95, f32[16,1,32,1408]{3,2,0,1:T(8,128)} %fusion.8, bf16[64,1,32,2048]{3,2,1,0:T(8,128)(2,1)} %all-to-all-done.3, s32[]{:T(128)S(6)} %select_n.35), kind=kOutput, calls=%fused_computation.14 | convolution fusion | flops 5910953984 | bytes 18612228 | tf_op jit(solution)/shard_map/sekf,efd->sekd/dot_general | solution.py:76
  277.3 2.9 collective-permute-start.1
  280.2 6.6 %convolution_convert_fusion.1 = bf16[256,2048]{1,0:T(8,128)(2,1)} fusion(bf16[704,2048]{1,0:T(8,128)(2,1)S(1)} %copy-done, bf16[2048,704]{0,1:T(8,128)(2,1)} %param.20, bf16[256,2048]{0,1:T(8,128)(2,1)} %copy-done.1, f32[256,704]{0,1:T(8,128)} %fusion.55), kind=kOutput, calls=%fused_computation.18 | convolution fusion | flops 1478000640 | bytes 8585216 | tf_op jit(solution)/shard_map/dot_general | solution.py:141
  289.7 5.7 %all-to-all-start.1 = ((bf16[4,256,512]{2,1,0:T(8,128)(2,1)}), bf16[4,256,512]{2,1,0:T(8,128)(2,1)}, u32[]{:S(2)}, u32[]{:S(2)}) async-start(bf16[4,256,512]{2,1,0:T(8,128)(2,1)} %bitcast.149), calls=%async_computation.1 | async-start | bytes 2097152 | tf_op jit(solution)/shard_map/all_to_all | solution.py:62
  300.7 3.8 collective-permute-done.1
  306.4 9.2 %collective-permute-done.2 = bf16[16,1,32,512]{3,2,0,1:T(8,128)(2,1)} collective-permute-done((bf16[16,1,32,512]{3,2,0,1:T(8,128)(2,1)}, bf16[16,1,32,512]{3,2,0,1:T(8,128)(2,1)}, u32[]{:S(2)}, u32[]{:S(2)}) %collective-permute-start.2) | collective-permute-done | bytes 524320 | tf_op jit(solution)/shard_map/ppermute | solution.py:18
  318.4 12.4 %all-to-all-start.4 = ((bf16[64,1,32,512]{3,2,1,0:T(8,128)(2,1)}), bf16[64,1,32,512]{3,2,1,0:T(8,128)(2,1)}, u32[]{:S(2)}, u32[]{:S(2)}) async-start(bf16[64,1,32,512]{3,2,1,0:T(8,128)(2,1)} %bitcast_dynamic-update-slice_fusion.1), calls=%async_computation.4 | async-start | bytes 4194304 | tf_op jit(solution)/shard_map/all_to_all | solution.py:67
  334.5 47.6 %all-to-all-done.4 = bf16[64,1,32,512]{3,2,1,0:T(8,128)(2,1)} async-done(((bf16[64,1,32,512]{3,2,1,0:T(8,128)(2,1)}), bf16[64,1,32,512]{3,2,1,0:T(8,128)(2,1)}, u32[]{:S(2)}, u32[]{:S(2)}) %all-to-all-start.4) | async-done | bytes 2097184 | tf_op jit(solution)/shard_map/all_to_all | solution.py:67
  382.0 7.0 %gather_fusion = bf16[1024,512]{1,0:T(8,128)(2,1)} fusion(bf16[2048,512]{1,0:T(8,128)(2,1)} %bitcast.45, s32[1024]{0:T(1024)S(1)} %broadcast_clamp_fusion), kind=kCustom, calls=%fused_computation | custom fusion | bytes 2101248 | tf_op jit(solution)/shard_map/gather | solution.py:136
  389.0 2.8 reshape.151
  391.7 3.0 multiply_reduce_fusion
  (70 shorter events, 31.6 us)
Async XLA Ops:
  6.5 273.7 %copy-start = (bf16[704,2048]{1,0:T(8,128)(2,1)S(1)}, bf16[704,2048]{1,0:T(8,128)(2,1)}, u32[]{:S(2)}) copy-start(bf16[704,2048]{1,0:T(8,128)(2,1)} %param.21) | copy-start | bytes 8650756
  6.5 119.1 %all-gather.3.cloned.1.call-start = ((), (), s32[]{:S(2)}) async-start(), calls=%async_computation.5 | async-start | bytes 14417920 | tf_op jit(solution)/shard_map/all_gather | solution.py:47
  10.3 0.9 copy-start.3
  10.4 8.5 %copy-start.5 = (s32[256,4]{0,1:T(4,128)S(1)}, s32[256,4]{0,1:T(4,128)}, u32[]{:S(2)}) copy-start(s32[256,4]{0,1:T(4,128)} %param.15) | copy-start | bytes 12292
  12.5 28.2 %all-to-all-start = ((bf16[4,256,512]{1,2,0:T(8,128)(2,1)}), bf16[4,256,512]{1,2,0:T(8,128)(2,1)}, u32[]{:S(2)}, u32[]{:S(2)}) async-start(bf16[4,256,512]{1,2,0:T(8,128)(2,1)} %broadcast_in_dim.16), calls=%async_computation | async-start | bytes 2097152 | tf_op jit(solution)/shard_map/all_to_all | solution.py:31
  18.8 23.5 %copy-start.6 = (f32[2048]{0:T(1024)S(1)}, f32[2048]{0:T(1024)}, u32[]{:S(2)}) copy-start(f32[2048]{0:T(1024)} %param.12) | copy-start | bytes 24580
  40.7 3.2 copy-start.2
  43.9 5.8 %copy-start.1 = (bf16[256,2048]{0,1:T(8,128)(2,1)}, bf16[256,2048]{0,1:T(8,128)(2,1)S(1)}, u32[]{:S(2)}) copy-start(bf16[256,2048]{0,1:T(8,128)(2,1)S(1)} %fusion.29) | copy-start | bytes 3145732
  49.7 11.7 %copy-start.4 = (bf16[512,60]{0,1:T(8,128)(2,1)S(1)}, bf16[512,60]{0,1:T(8,128)(2,1)}, u32[]{:S(2)}) copy-start(bf16[512,60]{0,1:T(8,128)(2,1)} %param.13) | copy-start | bytes 184324
  49.7 197.1 %all-to-all-start.3 = ((bf16[64,1,32,2048]{3,2,1,0:T(8,128)(2,1)}), bf16[64,1,32,2048]{3,2,1,0:T(8,128)(2,1)}, u32[]{:S(2)}, u32[]{:S(2)}) async-start(bf16[64,1,32,2048]{3,2,1,0:T(8,128)(2,1)} %bitcast.148), calls=%async_computation.3 | async-start | bytes 16777216 | tf_op jit(solution)/shard_map/all_to_all | solution.py:131
  60.6 200.0 %all-gather.5.cloned.1.call-start = ((), (), s32[]{:S(2)}) async-start(), calls=%async_computation.6 | async-start | bytes 7208960 | tf_op jit(solution)/shard_map/all_gather | solution.py:111
  247.5 42.2 %all-to-all-start.2 = ((f32[4,256,60]{1,2,0:T(8,128)}), f32[4,256,60]{1,2,0:T(8,128)S(1)}, u32[]{:S(2)}, u32[]{:S(2)}) async-start(f32[4,256,60]{1,2,0:T(8,128)} %broadcast_in_dim.17), calls=%async_computation.2 | async-start | bytes 524288 | tf_op jit(solution)/shard_map/all_to_all | solution.py:31
  277.3 21.6 %collective-permute-start = (bf16[16,1,32,512]{3,2,0,1:T(8,128)(2,1)}, bf16[16,1,32,512]{3,2,0,1:T(8,128)(2,1)}, u32[]{:S(2)}, u32[]{:S(2)}) collective-permute-start(bf16[16,1,32,512]{3,2,0,1:T(8,128)(2,1)} %get-tuple-element.11), channel_id=1, source_target_pairs={{0,1},{1,0},{2,3},{3,2},{4,5},{5,4},{6,7},{7,6},{8,9},{9,8},{10,11... | collective-permute-start | bytes 1572872 | tf_op jit(solution)/shard_map/ppermute | solution.py:18
  277.3 27.3 %collective-permute-start.1 = (bf16[16,1,32,512]{3,2,0,1:T(8,128)(2,1)}, bf16[16,1,32,512]{3,2,0,1:T(8,128)(2,1)}, u32[]{:S(2)}, u32[]{:S(2)}) collective-permute-start(bf16[16,1,32,512]{3,2,0,1:T(8,128)(2,1)} %get-tuple-element.10), channel_id=1, source_target_pairs={{0,2},{1,3},{2,0},{3,1},{4,6},{5,7},{6,4},{7,5},{8,10},{9,11},{10,... | collective-permute-start | bytes 1572872 | tf_op jit(solution)/shard_map/ppermute | solution.py:18
  289.1 26.5 %collective-permute-start.2 = (bf16[16,1,32,512]{3,2,0,1:T(8,128)(2,1)}, bf16[16,1,32,512]{3,2,0,1:T(8,128)(2,1)}, u32[]{:S(2)}, u32[]{:S(2)}) collective-permute-start(bf16[16,1,32,512]{3,2,0,1:T(8,128)(2,1)} %get-tuple-element.9), channel_id=1, source_target_pairs={{0,3},{1,2},{2,1},{3,0},{4,7},{5,6},{6,5},{7,4},{8,11},{9,10},{10,... | collective-permute-start | bytes 1572872 | tf_op jit(solution)/shard_map/ppermute | solution.py:18
  289.7 28.7 %all-to-all-start.1 = ((bf16[4,256,512]{2,1,0:T(8,128)(2,1)}), bf16[4,256,512]{2,1,0:T(8,128)(2,1)}, u32[]{:S(2)}, u32[]{:S(2)}) async-start(bf16[4,256,512]{2,1,0:T(8,128)(2,1)} %bitcast.149), calls=%async_computation.1 | async-start | bytes 2097152 | tf_op jit(solution)/shard_map/all_to_all | solution.py:62
  306.4 24.7 %copy-start.7 = (bf16[2048]{0:T(1024)(128)(2,1)S(1)}, bf16[2048]{0:T(1024)(128)(2,1)}, u32[]{:S(2)}) copy-start(bf16[2048]{0:T(1024)(128)(2,1)} %param.14) | copy-start | bytes 12292
  318.4 63.6 %all-to-all-start.4 = ((bf16[64,1,32,512]{3,2,1,0:T(8,128)(2,1)}), bf16[64,1,32,512]{3,2,1,0:T(8,128)(2,1)}, u32[]{:S(2)}, u32[]{:S(2)}) async-start(bf16[64,1,32,512]{3,2,1,0:T(8,128)(2,1)} %bitcast_dynamic-update-slice_fusion.1), calls=%async_computation.4 | async-start | bytes 4194304 | tf_op jit(solution)/shard_map/all_to_all | solution.py:67
Sparse Core Ops, SparseCore 0:
  10.5 115.1 all-gather.2
  127.5 64.4 all-gather.4
